TPU v7x, 256 devices: a whole 4x4x8 slice. The times are simulated.
256 devices in a mesh: row: 16 (over x, y), col: 16 (over z, core).
Axes of the slice: x: 4, y: 4, z: 8, core: 2. Of those that a mesh axis runs over, the one named last changes fastest.
Arguments:
- inputs: bfloat16 [2048, 16384], P('col', 'row'), may hold values from -6 to 6
- weight: bfloat16 [16384, 16384], P('row', 'col'), may hold values from -0.046875 to 0.046875
- cotangent: bfloat16 [2048, 16384], P('row', 'col'), may hold values from -0.75 to 0.75
- scale_in: float32 [8, 16384], P(None, 'row'), may hold values from -4 to 4
- scale_out: float32 [8, 16384], P(None, 'col'), may hold values from -4 to 4
- member: int32 [2048], replicated, may hold values from 0 to 7
Outputs:
- input_grad: bfloat16 [2048, 16384], P('col', 'row')
- weight_grad: float32 [16384, 16384], P('row', 'col')
- in_factor_grad: float32 [8, 16384], P(None, 'row')
- out_factor_grad: float32 [8, 16384], P(None, 'col')
All inputs are finite; a program needn't handle non-finite values.
Results may differ from a plain program's by a relative error of at most 0.0049.
Values may be sent and summed in bfloat16 or wider, within the bound.
No kernel may reach another device: no remote copies, remote signals or barrier semaphores. Data moves between devices by JAX's collectives and lax.ppermute only.
A program may use at most 128 MiB of HBM per device.

v0:
```python
import jax
import jax.numpy as jnp
from jax import lax
from jax.sharding import PartitionSpec as P

highest = lax.Precision.HIGHEST


def from_everyone(value, axis):
    copies = jnp.broadcast_to(value, (lax.axis_size(axis), *value.shape))
    return lax.all_to_all(copies, axis, split_axis=0, concat_axis=0, tiled=True)


def of_everyone(value, axis):
    return from_everyone(value, axis).sum(axis=0)


def gathered_total(value, axis):
    return lax.all_gather(value, axis).sum(0)


def member_sums(one_hot, values):
    return jnp.dot(one_hot.T, values, precision=highest)


def local(inputs, weight, cotangent, scale_in, scale_out, member):
    n_members = scale_in.shape[0]
    one_hot = (member[:, None] == jnp.arange(n_members, dtype=jnp.int32)[None, :]).astype(
        jnp.float32
    )
    full_inputs = lax.all_gather(inputs, "col", axis=0, tiled=True)
    full_cot = lax.all_gather(cotangent, "row", axis=0, tiled=True)
    r_rows = jnp.dot(one_hot, scale_in, precision=highest)
    s_rows = jnp.dot(one_hot, scale_out, precision=highest)
    scaled_in = (full_inputs * r_rows).astype(jnp.bfloat16)
    scaled_cot = (full_cot * s_rows).astype(jnp.bfloat16)
    batch = scaled_in.shape[0]
    pre_part = jnp.dot(scaled_in, weight, preferred_element_type=jnp.float32)
    out_term = member_sums(one_hot, full_cot.astype(jnp.float32) * pre_part)
    out_factor_grad = of_everyone(out_term, "row")
    col_share = batch // lax.axis_size("col")
    col_start = lax.axis_index("col") * col_share
    back_part = lax.dot_general(
        scaled_cot, weight, (((1,), (1,)), ((), ())), preferred_element_type=jnp.float32
    )
    in_term = member_sums(one_hot, full_inputs.astype(jnp.float32) * back_part)
    in_factor_grad = gathered_total(in_term, "col")
    back_block = lax.psum_scatter(back_part, "col", scatter_dimension=0, tiled=True)
    r_block = lax.dynamic_slice_in_dim(r_rows, col_start, col_share, 0)
    input_grad = (back_block * r_block).astype(jnp.bfloat16)
    weight_grad = lax.dot_general(
        scaled_in, scaled_cot, (((0,), (0,)), ((), ())), preferred_element_type=jnp.float32
    )
    return (input_grad, weight_grad, in_factor_grad, out_factor_grad)


def solution(mesh):
    placed = (
        P("col", "row"),
        P("row", "col"),
        P("row", "col"),
        P(None, "row"),
        P(None, "col"),
        P(),
    )
    return jax.shard_map(
        local,
        mesh=mesh,
        in_specs=placed,
        out_specs=(P("col", "row"), P("row", "col"), P(None, "row"), P(None, "col")),
        check_vma=False,
    )
```

profile of v0, /device:TPU:2, one launch (start us, length us, event | category | flops | bytes accessed | tf_op | source)
XLA Modules:
  0.0 195.8 jit_solution(3907940686163401925)
XLA Ops:
  7.2 0.0 all-gather.4.cloned.1.call-start
  7.2 0.7 all-gather.4.cloned.1.call-update
  7.9 0.0 all-gather.6.cloned.1.call-start
  8.0 0.7 all-gather.6.cloned.1.call-update
  8.7 0.0 reduce-scatter.2.cloned.1.call-start
  8.7 61.1 %all-gather.4.cloned.1.call-done = bf16[2048,1024]{1,0:T(8,128)(2,1)} async-done(((bf16[128,1024]{1,0:T(8,128)(2,1)}), bf16[2048,1024]{1,0:T(8,128)(2,1)}) %all-gather.4.cloned.1.call-update) | async-done | bytes 4194320 | tf_op jit(solution)/shard_map/all_gather | solution.py:32
  69.8 5.6 %fusion = bf16[2048,1024]{1,0:T(8,128)(2,1)S(1)} fusion(bf16[2048,1024]{1,0:T(8,128)(2,1)} %all-gather.4.cloned.1.call-done, f32[8,1024]{1,0:T(8,128)} %param.10, s32[2048]{0:T(1024)} %param.11), kind=kOutput, calls=%fused_computation.4 | convolution fusion | flops 207634432 | bytes 8429568 | tf_op jit(solution)/shard_map/dot_general | solution.py:34
  75.4 2.0 copy-done.2
  77.4 7.1 %fusion.13 = f32[2048,1024]{1,0:T(8,128)} fusion(bf16[2048,1024]{1,0:T(8,128)(2,1)S(1)} %fusion, bf16[1024,1024]{1,0:T(8,128)(2,1)S(1)} %copy-done), kind=kOutput, calls=%fused_computation.18 | convolution fusion | flops 4294967296 | bytes 14680064 | tf_op jit(solution)/shard_map/dot_general | solution.py:43
  84.5 0.7 copy-done.4
  85.1 0.1 copy-done.5
  85.2 5.6 %fusion.4 = f32[2048,1024]{1,0:T(8,128)} fusion(f32[8,1024]{1,0:T(8,128)S(1)} %copy-done.5, s32[2048]{0:T(1024)S(1)} %copy-done.4), kind=kOutput, calls=%fused_computation.9 | convolution fusion | flops 201342976 | bytes 8429568 | tf_op jit(solution)/shard_map/dot_general | solution.py:33
  90.8 22.5 %all-gather.6.cloned.1.call-done = bf16[2048,1024]{1,0:T(8,128)(2,1)} async-done(((bf16[128,1024]{1,0:T(8,128)(2,1)}), bf16[2048,1024]{1,0:T(8,128)(2,1)}) %all-gather.6.cloned.1.call-update) | async-done | bytes 4194320 | tf_op jit(solution)/shard_map/all_gather | solution.py:31
  113.3 7.7 %fusion.9 = f32[2048,1024]{1,0:T(8,128)S(1)} fusion(bf16[1024,1024]{1,0:T(8,128)(2,1)S(1)} %copy-done, f32[2048,1024]{1,0:T(8,128)} %fusion.4, bf16[2048,1024]{1,0:T(8,128)(2,1)} %all-gather.6.cloned.1.call-done), kind=kOutput, calls=%fused_computation.16 | convolution fusion | flops 4301258752 | bytes 23068672 | tf_op jit(solution)/shard_map/dot_general | solution.py:38
  121.0 3.4 %fusion.1 = f32[8,1024]{1,0:T(8,128)S(1)} fusion(f32[2048,1024]{1,0:T(8,128)S(1)} %fusion.9, bf16[2048,1024]{1,0:T(8,128)(2,1)S(1)} %copy-done.1, s32[2048]{0:T(1024)S(1)} %copy-done.4), kind=kOutput, calls=%fused_computation.5 | convolution fusion | flops 205537280 | bytes 12623872 | tf_op jit(solution)/shard_map/dot_general | solution.py:23
  124.5 0.9 broadcast_in_dim.2
  125.3 7.3 %all-to-all-start = ((f32[16,8,1024]{2,1,0:T(8,128)}), f32[16,8,1024]{2,1,0:T(8,128)S(1)}, u32[]{:S(2)}, u32[]{:S(2)}) async-start(f32[16,8,1024]{2,1,0:T(8,128)} %broadcast_in_dim.2), calls=%async_computation.1 | async-start | bytes 1048576 | tf_op jit(solution)/shard_map/all_to_all | solution.py:11
  132.6 12.9 %fusion.11 = f32[1024,1024]{1,0:T(8,128)} fusion(bf16[2048,1024]{1,0:T(8,128)(2,1)} %copy-done.2, f32[2048,1024]{1,0:T(8,128)} %fusion.4, bf16[2048,1024]{1,0:T(8,128)(2,1)} %all-gather.6.cloned.1.call-done), kind=kOutput, calls=%fused_computation.17 | convolution fusion | flops 4301258752 | bytes 20971520 | tf_op jit(solution)/shard_map/dot_general | solution.py:51
  145.5 5.9 %fusion.3 = f32[8,1024]{1,0:T(8,128)S(1)} fusion(f32[2048,1024]{1,0:T(8,128)} %fusion.13, bf16[2048,1024]{1,0:T(8,128)(2,1)S(1)} %copy-done.3, s32[2048]{0:T(1024)S(1)} %copy-done.4), kind=kOutput, calls=%fused_computation.7 | convolution fusion | flops 205537280 | bytes 12623872 | tf_op jit(solution)/shard_map/dot_general | solution.py:23
  151.4 18.8 %all-gather = f32[128,1024]{1,0:T(8,128)S(1)} all-gather(f32[8,1024]{1,0:T(8,128)S(1)} %fusion.3), channel_id=2, replica_groups=mesh['row'=16,'col'=16] {'col'}, dimensions={0}, use_global_device_ids=true | all-gather | bytes 557056 | tf_op jit(solution)/shard_map/all_gather | solution.py:19
  170.2 0.6 bitcast_reduce_fusion
  170.9 0.6 reduce_sum.19
  171.5 15.8 %reduce-scatter.2.cloned.1.call-done = f32[128,1024]{1,0:T(8,128)} async-done(((f32[2048,1024]{1,0:T(8,128)}), f32[128,1024]{1,0:T(8,128)}) %reduce-scatter.2.cloned.1.call-update) | async-done | bytes 524304 | tf_op jit(solution)/shard_map/reduce_scatter | solution.py:48
  187.4 2.0 %multiply_convert_fusion = bf16[128,1024]{1,0:T(8,128)(2,1)} fusion(f32[128,1024]{1,0:T(8,128)} %reduce-scatter.2.cloned.1.call-done, f32[2048,1024]{1,0:T(8,128)} %fusion.4, s32[]{:T(128)S(6)} %select_n.3), kind=kLoop, calls=%fused_computation.11 | loop fusion | flops 262144 | bytes 1310724 | tf_op jit(solution)/shard_map/convert_element_type | solution.py:50
  (11 shorter events, 0.0 us)
Async XLA Ops:
  7.2 70.2 %copy-start = (bf16[1024,1024]{1,0:T(8,128)(2,1)S(1)}, bf16[1024,1024]{1,0:T(8,128)(2,1)}, u32[]{:S(2)}) copy-start(bf16[1024,1024]{1,0:T(8,128)(2,1)} %param.7) | copy-start | bytes 6291460
  7.2 62.6 %all-gather.4.cloned.1.call-start = ((), (), s32[]{:S(2)}) async-start(), calls=%async_computation.2 | async-start | bytes 4456448 | tf_op jit(solution)/shard_map/all_gather | solution.py:32
  7.9 105.4 %all-gather.6.cloned.1.call-start = ((), (), s32[]{:S(2)}) async-start(), calls=%async_computation.4 | async-start | bytes 4456448 | tf_op jit(solution)/shard_map/all_gather | solution.py:31
  8.7 178.7 %reduce-scatter.2.cloned.1.call-start = ((), (), s32[]{:S(2)}) async-start(), calls=%async_computation.3 | async-start | bytes 8912896 | tf_op jit(solution)/shard_map/reduce_scatter | solution.py:48
  75.4 2.0 %copy-start.2 = (bf16[2048,1024]{1,0:T(8,128)(2,1)}, bf16[2048,1024]{1,0:T(8,128)(2,1)S(1)}, u32[]{:S(2)}) copy-start(bf16[2048,1024]{1,0:T(8,128)(2,1)S(1)} %fusion) | copy-start | bytes 12582916
  84.4 0.7 copy-start.4
  84.4 0.8 copy-start.5
  113.3 7.7 %copy-start.1 = (bf16[2048,1024]{1,0:T(8,128)(2,1)S(1)}, bf16[2048,1024]{1,0:T(8,128)(2,1)}, u32[]{:S(2)}) copy-start(bf16[2048,1024]{1,0:T(8,128)(2,1)} %all-gather.4.cloned.1.call-done) | copy-start | bytes 12582916
  125.3 45.5 %all-to-all-start = ((f32[16,8,1024]{2,1,0:T(8,128)}), f32[16,8,1024]{2,1,0:T(8,128)S(1)}, u32[]{:S(2)}, u32[]{:S(2)}) async-start(f32[16,8,1024]{2,1,0:T(8,128)} %broadcast_in_dim.2), calls=%async_computation.1 | async-start | bytes 1048576 | tf_op jit(solution)/shard_map/all_to_all | solution.py:11
  132.6 12.9 %copy-start.3 = (bf16[2048,1024]{1,0:T(8,128)(2,1)S(1)}, bf16[2048,1024]{1,0:T(8,128)(2,1)}, u32[]{:S(2)}) copy-start(bf16[2048,1024]{1,0:T(8,128)(2,1)} %all-gather.6.cloned.1.call-done) | copy-start | bytes 12582916
Sparse Core Ops, SparseCore 0:
  10.4 59.3 all-gather.3
  71.7 41.6 all-gather.5
  115.9 71.4 reduce-scatter.1
where the time goes:
time: 196 us
  waiting for transfers between devices  101 us (52%)
  matrix products  48.2 us (25%)
  blocking collectives  18.8 us (10%)
  between operations  13.8 us (7%)
  starting transfers between devices  7.39 us (4%)
  local copies, waits for them, and re-layouts  3.59 us (2%)
  other arithmetic  3.25 us (2%)
    all_gather x1, waiting for transfers between devices, local(): full_cot = lax.all_gather(cotangent, 'row', axis=0, tiled=True)  61.1 us
    all_gather x1, waiting for transfers between devices, local(): full_inputs = lax.all_gather(inputs, 'col', axis=0, tiled=True)  22.5 us
    all_gather x1, blocking collectives, gathered_total(): return lax.all_gather(value, axis).sum(0)  18.8 us
    reduce_scatter x1, waiting for transfers between devices, local(): lax.psum_scatter(back_part, 'col', scatter_dimension=0, tiled=True)  15.8 us
    dot_general x1, matrix products, local(): lax.dot_general(scaled_in, scaled_cot, (((0,), (0,)), ((), ())), preferre...  12.9 us
    dot_general x2, matrix products, member_sums(): return jnp.dot(one_hot.T, values, precision=highest)  9.29 us
    dot_general x1, matrix products, local(): pre_part = jnp.dot(scaled_in, weight, preferred_element_type=jnp.float32)  7.7 us
    all_to_all x1, starting transfers between devices, from_everyone(): return lax.all_to_all(copies, axis, split_axis=0, concat_axis=0, tiled=True)  7.28 us
  transfers between devices with their start and end apart: 4, of which 3 were waited for; matrix products, arithmetic and copies ran while one was open for 26% of the time, Pallas kernels for 0%

commit v1 on v0

--- a/solution.py
+++ b/solution.py
@@ -29,7 +29,9 @@
         jnp.float32
     )
     full_inputs = lax.all_gather(inputs, "col", axis=0, tiled=True)
-    full_cot = lax.all_gather(cotangent, "row", axis=0, tiled=True)
+    full_cot = jnp.concatenate(
+        lax.all_to_all(jnp.stack([cotangent] * lax.axis_size("row")), "row", 0, 0), axis=0
+    )
     r_rows = jnp.dot(one_hot, scale_in, precision=highest)
     s_rows = jnp.dot(one_hot, scale_out, precision=highest)
     scaled_in = (full_inputs * r_rows).astype(jnp.bfloat16)

time: 196 us -> 164 us (0.84)
  waiting for transfers between devices: 101 us -> 7.34 us
  blocking collectives: 18.8 us -> 79.3 us
  local copies, waits for them, and re-layouts: 3.59 us -> 7.11 us
    all_gather x1 -> x0, waiting for transfers between devices: 61.1 us -> none  [local(): full_cot = lax.all_gather(cotangent, 'row', axis=0, tiled=True)]
    all_to_all x0 -> x1, blocking collectives: none -> 56.6 us  [local(): lax.all_to_all(jnp.stack([cotangent] * lax.axis_size('row')), 'row', 0, 0)]
    all_gather x1, waiting for transfers between devices: 22.5 us -> 0.01 us  [local(): full_inputs = lax.all_gather(inputs, 'col', axis=0, tiled=True)]
    reduce_scatter x1, waiting for transfers between devices: 15.8 us -> 6.64 us  [local(): lax.psum_scatter(back_part, 'col', scatter_dimension=0, tiled=True)]
    all_gather x1, blocking collectives: 18.8 us -> 22.6 us  [gathered_total(): return lax.all_gather(value, axis).sum(0)]
    unnamed x12 -> x16, local copies, waits for them, and re-layouts: 2.71 us -> 4.75 us
  transfers between devices with their start and end apart: 4 -> 3, of which waited for: 3 -> 1; matrix products, arithmetic and copies ran while one was open for 26% -> 31% of each run, Pallas kernels for 0% -> 0%
where the time goes in v1:
time: 164 us
  blocking collectives  79.3 us (48%)
  matrix products  46.8 us (29%)
  between operations  14.1 us (9%)
  waiting for transfers between devices  7.34 us (4%)
  local copies, waits for them, and re-layouts  7.11 us (4%)
  starting transfers between devices  5.95 us (4%)
  other arithmetic  3.25 us (2%)
    all_to_all x1, blocking collectives, local(): lax.all_to_all(jnp.stack([cotangent] * lax.axis_size('row')), 'row', 0, 0)  56.6 us
    all_gather x1, blocking collectives, gathered_total(): return lax.all_gather(value, axis).sum(0)  22.6 us
    dot_general x1, matrix products, local(): lax.dot_general(scaled_in, scaled_cot, (((0,), (0,)), ((), ())), preferre...  13 us
    dot_general x2, matrix products, member_sums(): return jnp.dot(one_hot.T, values, precision=highest)  9.24 us
    dot_general x1, matrix products, local(): pre_part = jnp.dot(scaled_in, weight, preferred_element_type=jnp.float32)  7.7 us
    dot_general x1, matrix products, local(): lax.dot_general(scaled_cot, weight, (((1,), (1,)), ((), ())), preferred_e...  7.13 us
    reduce_scatter x1, waiting for transfers between devices, local(): lax.psum_scatter(back_part, 'col', scatter_dimension=0, tiled=True)  6.64 us
    all_to_all x1, starting transfers between devices, from_everyone(): return lax.all_to_all(copies, axis, split_axis=0, concat_axis=0, tiled=True)  5.87 us
  transfers between devices with their start and end apart: 3, of which 1 were waited for; matrix products, arithmetic and copies ran while one was open for 31% of the time, Pallas kernels for 0%

profile of v1, /device:TPU:2, one launch (start us, length us, event | category | flops | bytes accessed | tf_op | source)
XLA Modules:
  0.0 163.8 jit_solution(17665908159831454993)
XLA Ops:
  7.2 0.0 copy-start
  7.2 0.0 all-gather.3.cloned.1.call-start
  7.2 0.7 all-gather.3.cloned.1.call-update
  7.9 0.0 reduce-scatter.2.cloned.1.call-start
  8.0 1.5 stack.2
  9.5 56.6 %all_to_all.10 = bf16[16,128,1024]{2,1,0:T(8,128)(2,1)S(1)} all-to-all(bf16[16,128,1024]{2,1,0:T(8,128)(2,1)S(1)} %stack.2), channel_id=1, replica_groups=mesh['row'=16,'col'=16] {'row'}, dimensions={0} | all-to-all | bytes 8388608 | tf_op jit(solution)/shard_map/all_to_all | solution.py:33
  66.1 2.0 %copy-done.1 = bf16[16,128,1024]{2,1,0:T(8,128)(2,1)} copy-done((bf16[16,128,1024]{2,1,0:T(8,128)(2,1)}, bf16[16,128,1024]{2,1,0:T(8,128)(2,1)S(1)}, u32[]{:S(2)}) %copy-start.1) | copy-done | bytes 4194328
  68.1 4.0 %fusion.2 = bf16[2048,1024]{1,0:T(8,128)(2,1)S(1)} fusion(bf16[2048,1024]{1,0:T(8,128)(2,1)S(1)} %bitcast.10, f32[8,1024]{1,0:T(8,128)S(1)} %copy-done.6, s32[2048]{0:T(1024)S(1)} %copy-done.5), kind=kOutput, calls=%fused_computation.6 | convolution fusion | flops 207634432 | bytes 8429568 | tf_op jit(solution)/shard_map/dot_general | solution.py:36
  72.2 2.0 %copy-done.3 = bf16[2048,1024]{1,0:T(8,128)(2,1)} copy-done((bf16[2048,1024]{1,0:T(8,128)(2,1)}, bf16[2048,1024]{1,0:T(8,128)(2,1)S(1)}, u32[]{:S(2)}) %copy-start.3) | copy-done | bytes 4194328
  74.2 7.1 %fusion.13 = f32[2048,1024]{1,0:T(8,128)} fusion(bf16[2048,1024]{1,0:T(8,128)(2,1)S(1)} %fusion.2, bf16[1024,1024]{1,0:T(8,128)(2,1)S(1)} %copy-done), kind=kOutput, calls=%fused_computation.18 | convolution fusion | flops 4294967296 | bytes 14680064 | tf_op jit(solution)/shard_map/dot_general | solution.py:45
  81.3 0.0 reduce-scatter.2.cloned.1.call-update
  81.3 0.7 copy-done.7
  82.0 5.6 %fusion.4 = f32[2048,1024]{1,0:T(8,128)} fusion(f32[8,1024]{1,0:T(8,128)S(1)} %copy-done.7, s32[2048]{0:T(1024)S(1)} %copy-done.5), kind=kOutput, calls=%fused_computation.9 | convolution fusion | flops 201342976 | bytes 8429568 | tf_op jit(solution)/shard_map/dot_general | solution.py:35
  87.7 7.7 %fusion.9 = f32[2048,1024]{1,0:T(8,128)S(1)} fusion(bf16[1024,1024]{1,0:T(8,128)(2,1)S(1)} %copy-done, f32[2048,1024]{1,0:T(8,128)} %fusion.4, bf16[2048,1024]{1,0:T(8,128)(2,1)} %all-gather.3.cloned.1.call-done), kind=kOutput, calls=%fused_computation.16 | convolution fusion | flops 4301258752 | bytes 23068672 | tf_op jit(solution)/shard_map/dot_general | solution.py:40
  95.4 3.4 %fusion.3 = f32[8,1024]{1,0:T(8,128)S(1)} fusion(f32[2048,1024]{1,0:T(8,128)S(1)} %fusion.9, bf16[2048,1024]{1,0:T(8,128)(2,1)S(1)} %bitcast.11, s32[2048]{0:T(1024)S(1)} %copy-done.5), kind=kOutput, calls=%fused_computation.7 | convolution fusion | flops 205537280 | bytes 12623872 | tf_op jit(solution)/shard_map/dot_general | solution.py:23
  98.8 0.9 broadcast_in_dim.2
  99.7 5.9 %all-to-all-start.1 = ((f32[16,8,1024]{2,1,0:T(8,128)}), f32[16,8,1024]{2,1,0:T(8,128)S(1)}, u32[]{:S(2)}, u32[]{:S(2)}) async-start(f32[16,8,1024]{2,1,0:T(8,128)} %broadcast_in_dim.2), calls=%async_computation.2 | async-start | bytes 1048576 | tf_op jit(solution)/shard_map/all_to_all | solution.py:11
  105.6 13.0 %fusion.11 = f32[1024,1024]{1,0:T(8,128)} fusion(bf16[2048,1024]{1,0:T(8,128)(2,1)} %copy-done.3, f32[2048,1024]{1,0:T(8,128)} %fusion.4, bf16[2048,1024]{1,0:T(8,128)(2,1)} %all-gather.3.cloned.1.call-done), kind=kOutput, calls=%fused_computation.17 | convolution fusion | flops 4301258752 | bytes 20971520 | tf_op jit(solution)/shard_map/dot_general | solution.py:53
  118.6 5.8 %fusion.1 = f32[8,1024]{1,0:T(8,128)S(1)} fusion(f32[2048,1024]{1,0:T(8,128)} %fusion.13, bf16[2048,1024]{1,0:T(8,128)(2,1)S(1)} %copy-done.4, s32[2048]{0:T(1024)S(1)} %copy-done.5), kind=kOutput, calls=%fused_computation.5 | convolution fusion | flops 205537280 | bytes 12623872 | tf_op jit(solution)/shard_map/dot_general | solution.py:23
  124.4 22.6 %all-gather = f32[128,1024]{1,0:T(8,128)S(1)} all-gather(f32[8,1024]{1,0:T(8,128)S(1)} %fusion.1), channel_id=2, replica_groups=mesh['row'=16,'col'=16] {'col'}, dimensions={0}, use_global_device_ids=true | all-gather | bytes 557056 | tf_op jit(solution)/shard_map/all_gather | solution.py:19
  147.1 0.6 bitcast_reduce_fusion
  147.7 0.6 reduce_sum.19
  148.4 6.6 %reduce-scatter.2.cloned.1.call-done = f32[128,1024]{1,0:T(8,128)} async-done(((f32[2048,1024]{1,0:T(8,128)}), f32[128,1024]{1,0:T(8,128)}) %reduce-scatter.2.cloned.1.call-update) | async-done | bytes 524304 | tf_op jit(solution)/shard_map/reduce_scatter | solution.py:50
  155.0 2.0 %multiply_convert_fusion = bf16[128,1024]{1,0:T(8,128)(2,1)} fusion(f32[128,1024]{1,0:T(8,128)} %reduce-scatter.2.cloned.1.call-done, f32[2048,1024]{1,0:T(8,128)} %fusion.4, s32[]{:T(128)S(6)} %select_n.3), kind=kLoop, calls=%fused_computation.11 | loop fusion | flops 262144 | bytes 1310724 | tf_op jit(solution)/shard_map/convert_element_type | solution.py:52
  (14 shorter events, 0.0 us)
Async XLA Ops:
  7.2 67.0 %copy-start = (bf16[1024,1024]{1,0:T(8,128)(2,1)S(1)}, bf16[1024,1024]{1,0:T(8,128)(2,1)}, u32[]{:S(2)}) copy-start(bf16[1024,1024]{1,0:T(8,128)(2,1)} %param.7) | copy-start | bytes 6291460
  7.2 80.5 %all-gather.3.cloned.1.call-start = ((), (), s32[]{:S(2)}) async-start(), calls=%async_computation.4 | async-start | bytes 4456448 | tf_op jit(solution)/shard_map/all_gather | solution.py:31
  7.9 147.1 %reduce-scatter.2.cloned.1.call-start = ((), (), s32[]{:S(2)}) async-start(), calls=%async_computation.3 | async-start | bytes 8912896 | tf_op jit(solution)/shard_map/reduce_scatter | solution.py:50
  9.4 58.7 %copy-start.5 = (s32[2048]{0:T(1024)S(1)}, s32[2048]{0:T(1024)}, u32[]{:S(2)}) copy-start(s32[2048]{0:T(1024)} %param.11) | copy-start | bytes 24580
  9.5 58.7 %copy-start.6 = (f32[8,1024]{1,0:T(8,128)S(1)}, f32[8,1024]{1,0:T(8,128)}, u32[]{:S(2)}) copy-start(f32[8,1024]{1,0:T(8,128)} %param.10) | copy-start | bytes 98308
  66.1 2.0 %copy-start.1 = (bf16[16,128,1024]{2,1,0:T(8,128)(2,1)}, bf16[16,128,1024]{2,1,0:T(8,128)(2,1)S(1)}, u32[]{:S(2)}) copy-start(bf16[16,128,1024]{2,1,0:T(8,128)(2,1)S(1)} %all_to_all.10) | copy-start | bytes 12582916
  72.2 2.0 %copy-start.3 = (bf16[2048,1024]{1,0:T(8,128)(2,1)}, bf16[2048,1024]{1,0:T(8,128)(2,1)S(1)}, u32[]{:S(2)}) copy-start(bf16[2048,1024]{1,0:T(8,128)(2,1)S(1)} %fusion.2) | copy-start | bytes 12582916
  81.3 0.8 copy-start.7
  87.7 7.7 %copy-start.2 = (bf16[16,128,1024]{2,1,0:T(8,128)(2,1)S(1)}, bf16[16,128,1024]{2,1,0:T(8,128)(2,1)}, u32[]{:S(2)}) copy-start(bf16[16,128,1024]{2,1,0:T(8,128)(2,1)} %copy-done.1) | copy-start | bytes 12582916
  99.7 48.0 %all-to-all-start.1 = ((f32[16,8,1024]{2,1,0:T(8,128)}), f32[16,8,1024]{2,1,0:T(8,128)S(1)}, u32[]{:S(2)}, u32[]{:S(2)}) async-start(f32[16,8,1024]{2,1,0:T(8,128)} %broadcast_in_dim.2), calls=%async_computation.2 | async-start | bytes 1048576 | tf_op jit(solution)/shard_map/all_to_all | solution.py:11
  105.6 13.1 %copy-start.4 = (bf16[2048,1024]{1,0:T(8,128)(2,1)S(1)}, bf16[2048,1024]{1,0:T(8,128)(2,1)}, u32[]{:S(2)}) copy-start(bf16[2048,1024]{1,0:T(8,128)(2,1)} %all-gather.3.cloned.1.call-done) | copy-start | bytes 12582916
Sparse Core Ops, SparseCore 0:
  9.8 44.9 all-gather.2
  81.4 73.5 reduce-scatter.1
